TPU v7x, 32 devices: a whole 2x2x4 slice. The times are simulated.
32 devices in a mesh: cells: 32 (over z, y, x, core).
Axes of the slice: x: 2, y: 2, z: 4, core: 2. Of those that a mesh axis runs over, the one named last changes fastest.
Arguments:
- field: float32 [9, 55, 32768], P(None, None, 'cells'), may hold values from -6 to 6
- cell_area: float32 [32768], P('cells'), may hold values from 0.5 to 2
- dv_edge: float32 [103424], P('cells'), may hold values from 0.6 to 1.6
- dc_edge: float32 [103424], P('cells'), may hold values from 0.6 to 1.6
- cells_on_edge: int32 [2, 103424], P(None, 'cells'), may hold values from 0 to 1407, as said below
- edges_on_cell: int32 [6, 32768], P(None, 'cells'), may hold values from 0 to 3231, as said below
- send_cells: int32 [6, 2048], P(None, 'cells'), may hold values from 0 to 1023
- level_coef: float32 [55], replicated, may hold values from 0.005 to 0.02
Outputs:
- tendency: float32 [9, 55, 32768], P(None, None, 'cells')
Inputs may be any that keep to these rules, and one draw needn't show every extreme that they name: `cells_on_edge`: the blocks tile one periodic hexagonal mesh, each a parallelogram of 64 by 16 cells; block b borders b + 1 and b - 1 along the first direction, b + 16 and b - 16 along the second, and b + 15 and b - 15 at one cell each, all modulo 32. Every edge with a cell in a block is listed once in that block, with the same dv_edge and dc_edge wherever it is listed, plus one extra entry that no cell names. Cells and edges are numbered in random order in each block. `edges_on_cell`: each cell names six distinct edges of its block.
All inputs are finite; a program needn't handle non-finite values.
Results may differ from a plain program's by a relative error of at most 0.00005.
Values sent between devices are 32-bit elements; how exact they have to be, the bound alone decides.
A program may use at most 128 MiB of HBM per device.

v0:
```python
import functools

import jax
import jax.numpy as jnp
from jax import lax
from jax.experimental import pallas as pl
from jax.experimental.pallas import tpu as pltpu
from jax.sharding import PartitionSpec as P

CELLS_Y = 16
BLOCK_ROW = 16
OFFSETS = (1, -1, BLOCK_ROW, -BLOCK_ROW, BLOCK_ROW - 1, 1 - BLOCK_ROW)
LANES = 128
CHUNKS = 2


def up(value, step):
    return -(-value // step) * step


def slots(length):
    side = CELLS_Y
    counts = (side, side, length, length, 8, 8)
    order = (2, 3, 0, 1, 4, 5)
    base = [0] * 6
    at = 0
    for k in order:
        base[k] = at
        at += counts[k]
    return tuple(base), counts, at


def prepare_kernel(
    dv_hbm, dc_hbm, ends_hbm, edges_hbm, send_hbm, area_hbm, near_ref, coef_ref, cols_ref,
    weight, packed, index, dv_ref, dc_ref, ends_ref, edges_ref, send_ref, area_ref, sems,
):
    pairs = (
        (dv_hbm, dv_ref), (dc_hbm, dc_ref), (ends_hbm, ends_ref), (edges_hbm, edges_ref),
        (send_hbm, send_ref), (area_hbm, area_ref),
    )
    loads = [pltpu.make_async_copy(a, b, sems.at[i]) for i, (a, b) in enumerate(pairs)]
    for load in loads:
        load.start()
    edge_count = ends_ref.shape[1]
    cell_count = edges_ref.shape[1]
    length = send_ref.shape[1]
    base, counts, _ = slots(length)
    tables = weight.shape[1] // LANES
    weight[...] = jnp.zeros_like(weight)
    packed[...] = jnp.zeros_like(packed)
    index[...] = jnp.zeros_like(index)
    for load in loads:
        load.wait()
    for k in range(tables):
        part = slice(k * LANES, min((k + 1) * LANES, edge_count))
        weight[0, part] = dv_ref[part] / dc_ref[part]
    packed[:, :edge_count] = ends_ref[0:1, :] + ends_ref[1:2, :] * 4096
    index[0:6, :] = edges_ref[...]
    row = lax.broadcasted_iota(jnp.int32, (8, LANES), 0)
    lane = lax.broadcasted_iota(jnp.int32, (8, LANES), 1)
    for tile in range(cell_count // LANES):
        here = slice(tile * LANES, (tile + 1) * LANES)
        wanted = index[:, here]
        high = wanted >> 7
        low = wanted & 127
        w = jnp.zeros((8, LANES), jnp.float32)
        p = jnp.zeros((8, LANES), jnp.int32)
        for k in range(tables):
            part = slice(k * LANES, (k + 1) * LANES)
            wk = jnp.broadcast_to(weight[0:1, part], (8, LANES))
            pk = jnp.broadcast_to(packed[0:1, part], (8, LANES))
            hit = high == k
            w = jnp.where(hit, jnp.take_along_axis(wk, low, axis=1), w)
            p = jnp.where(hit, jnp.take_along_axis(pk, low, axis=1), p)
        first = p & 4095
        second = p >> 12
        other = jnp.where(first == lane + tile * LANES, second, first)
        away = other - cell_count
        place = jnp.zeros((8, LANES), jnp.int32)
        for k in range(6):
            inside = (away >= k * length) & (away < (k + 1) * length)
            place = jnp.where(inside, away - k * length + base[k], place)
        near = jnp.where(away < 0, other, cell_count + place)
        share = w / jnp.broadcast_to(area_ref[here], (8, LANES))
        share = jnp.where(row < 6, share, 0.0)
        total = jnp.sum(share, axis=0, keepdims=True)
        near_ref[:, here] = jnp.where(row < 6, near, -1)
        coef_ref[:, here] = jnp.where(row == 6, total, share)
    for k in range(6):
        rows = lax.broadcasted_iota(jnp.int32, (counts[k], length), 0)
        columns = lax.broadcasted_iota(jnp.int32, (counts[k], length), 1)
        ids = send_ref[k : k + 1, :].astype(jnp.float32)
        column = jnp.sum(jnp.where(rows == columns, ids, 0.0), axis=1, keepdims=True)
        cols_ref[base[k] : base[k] + counts[k], :] = jnp.broadcast_to(
            column, (counts[k], LANES)
        ).astype(jnp.int32)


def split(values):
    high = values.astype(jnp.bfloat16)
    low = (values - high.astype(jnp.float32)).astype(jnp.bfloat16)
    return high, low


def main_kernel(
    devices, length, field_ref, near_ref, coef_ref, cols_ref, out_ref,
    landed, flat, first, matrix, rim, triple, selector, outgoing, incoming,
    load_sem, send_sem, recv_sem,
):
    fields_n, levels_n, cell_count = field_ref.shape
    stride = up(levels_n, 8)
    chunk = flat.shape[0] // CHUNKS
    halo = rim.shape[0] // 3
    base, counts, used = slots(length)
    me = lax.axis_index("cells")
    targets = [lax.rem(me + (o + devices), devices) for o in OFFSETS]

    loads = [
        pltpu.make_async_copy(field_ref.at[f], landed.at[f], load_sem.at[f])
        for f in range(fields_n)
    ]
    for load in loads:
        load.start()

    barrier = pltpu.get_barrier_semaphore()
    for target in targets:
        pl.semaphore_signal(
            barrier, inc=1, device_id=(target,), device_id_type=pl.DeviceIdType.MESH
        )

    lane = lax.broadcasted_iota(jnp.int32, (used, LANES), 1)
    for tile in range(cell_count // LANES):
        hit = cols_ref[...] == lane + tile * LANES
        ones = jnp.where(hit, 1.0, 0.0).astype(jnp.bfloat16)
        selector[:, tile * LANES : (tile + 1) * LANES] = ones
        at = cell_count + tile * LANES
        selector[:, at : at + LANES] = ones
    for lap in range(2):
        for c in range(CHUNKS):
            incoming[lap, c, used:, :] = jnp.zeros((halo - used, chunk), jnp.float32)
    rows = flat.shape[0]
    end = fields_n * stride
    if rows > end:
        flat[end:, :] = jnp.zeros((rows - end, cell_count), jnp.float32)
    if stride > levels_n:
        for f in range(fields_n):
            at = (f + 1) * stride - 8
            flat[at : at + 8, :] = jnp.zeros((8, cell_count), jnp.float32)

    def spread(values, c):
        high, low = split(values)
        triple[c, :, :cell_count] = high
        triple[c, :, cell_count : 2 * cell_count] = low
        triple[c, :, 2 * cell_count :] = high

    def copies(lap, c):
        return [
            pltpu.make_async_remote_copy(
                src_ref=outgoing.at[lap, c, pl.ds(base[k], counts[k])],
                dst_ref=incoming.at[lap, c, pl.ds(base[k], counts[k])],
                send_sem=send_sem.at[lap, c, k],
                recv_sem=recv_sem.at[lap, c, k],
                device_id=(targets[k],),
                device_id_type=pl.DeviceIdType.MESH,
            )
            for k in (2, 3, 4, 5, 0, 1)
        ]

    def send(lap, c):
        outgoing[lap, c] = lax.dot_general(
            selector[...],
            triple[c, :, : 2 * cell_count],
            (((1,), (1,)), ((), ())),
            preferred_element_type=jnp.float32,
        )
        for copy in copies(lap, c):
            copy.start()

    def own(c):
        return jnp.dot(triple[c], matrix[...], preferred_element_type=jnp.float32)

    def outside(lap, c):
        for copy in copies(lap, c):
            copy.wait_recv()
        high, low = split(incoming[lap, c].T)
        lhs = jnp.concatenate([high, low, high], axis=1)
        return jnp.dot(lhs, rim[...], preferred_element_type=jnp.float32)

    loaded = 0
    for c in range(CHUNKS):
        need = min(fields_n, -(-((c + 1) * chunk) // stride))
        for f in range(loaded, need):
            loads[f].wait()
            flat[f * stride : f * stride + levels_n, :] = landed[f]
        loaded = max(loaded, need)
        spread(flat[c * chunk : (c + 1) * chunk, :], c)
        if c == 0:
            pl.semaphore_wait(barrier, len(targets))
        send(0, c)

    ids = lax.broadcasted_iota(jnp.int32, (LANES, LANES), 0)

    def entries(start, tile):
        here = slice(tile * LANES, (tile + 1) * LANES)
        block = jnp.zeros((LANES, LANES), jnp.float32)
        for j in range(6):
            hit = ids == near_ref[j : j + 1, here] - start
            block = jnp.where(hit, coef_ref[j : j + 1, here], block)
        return split(block)

    def fill(r, carry):
        start = pl.multiple_of(r * LANES, LANES)
        for tile in range(cell_count // LANES):
            here = slice(tile * LANES, (tile + 1) * LANES)
            high, low = entries(start, tile)
            matrix[pl.ds(start, LANES), here] = high
            matrix[pl.ds(start + cell_count, LANES), here] = high
            matrix[pl.ds(start + 2 * cell_count, LANES), here] = low
        return carry

    lax.fori_loop(0, cell_count // LANES, fill, 0)
    for r in range(halo // LANES):
        for tile in range(cell_count // LANES):
            here = slice(tile * LANES, (tile + 1) * LANES)
            high, low = entries(cell_count + r * LANES, tile)
            rim[r * LANES : (r + 1) * LANES, here] = high
            rim[halo + r * LANES : halo + (r + 1) * LANES, here] = high
            rim[2 * halo + r * LANES : 2 * halo + (r + 1) * LANES, here] = low

    for c in range(CHUNKS):
        part = slice(c * chunk, (c + 1) * chunk)
        first[part, :] = own(c) - flat[part, :] * coef_ref[6:7, :]
        result = first[part, :] + outside(0, c)
        first[part, :] = result
        spread(result, c)
        send(1, c)
    for c in range(CHUNKS):
        part = slice(c * chunk, (c + 1) * chunk)
        out_ref[part, :] = own(c) - first[part, :] * coef_ref[6:7, :]
        out_ref[part, :] = out_ref[part, :] + outside(1, c)
    for lap in range(2):
        for c in range(CHUNKS):
            for copy in copies(lap, c):
                copy.wait_send()


def shards(
    devices, field, cell_area, dv_edge, dc_edge, cells_on_edge, edges_on_cell, send_cells,
    level_coef,
):
    length = send_cells.shape[1]
    fields_n, levels_n, cell_count = field.shape
    edge_count = dv_edge.shape[0]
    _, _, used = slots(length)
    halo = up(used, LANES)
    stride = up(levels_n, 8)
    rows = up(fields_n * stride, CHUNKS * LANES)
    chunk = rows // CHUNKS
    vmem = pl.BlockSpec(memory_space=pltpu.VMEM)
    hbm = pl.BlockSpec(memory_space=pltpu.HBM)
    near, coef, cols = pl.pallas_call(
        prepare_kernel,
        out_shape=(
            jax.ShapeDtypeStruct((8, cell_count), jnp.int32),
            jax.ShapeDtypeStruct((8, cell_count), jnp.float32),
            jax.ShapeDtypeStruct((used, LANES), jnp.int32),
        ),
        in_specs=[hbm] * 6,
        out_specs=(vmem,) * 3,
        scratch_shapes=[
            pltpu.VMEM((1, up(edge_count, LANES)), jnp.float32),
            pltpu.VMEM((1, up(edge_count, LANES)), jnp.int32),
            pltpu.VMEM((8, cell_count), jnp.int32),
            pltpu.VMEM(dv_edge.shape, jnp.float32),
            pltpu.VMEM(dc_edge.shape, jnp.float32),
            pltpu.VMEM(cells_on_edge.shape, jnp.int32),
            pltpu.VMEM(edges_on_cell.shape, jnp.int32),
            pltpu.VMEM(send_cells.shape, jnp.int32),
            pltpu.VMEM(cell_area.shape, jnp.float32),
            pltpu.SemaphoreType.DMA((6,)),
        ],
        compiler_params=pltpu.CompilerParams(vmem_limit_bytes=67043328),
        name="prepare",
    )(
        dv_edge,
        dc_edge,
        cells_on_edge,
        edges_on_cell,
        send_cells,
        cell_area,
    )
    second = pl.pallas_call(
        functools.partial(main_kernel, devices, length),
        out_shape=jax.ShapeDtypeStruct((rows, cell_count), jnp.float32),
        in_specs=[hbm, vmem, vmem, vmem],
        out_specs=vmem,
        scratch_shapes=[
            pltpu.VMEM((fields_n, levels_n, cell_count), jnp.float32),
            pltpu.VMEM((rows, cell_count), jnp.float32),
            pltpu.VMEM((rows, cell_count), jnp.float32),
            pltpu.VMEM((3 * cell_count, cell_count), jnp.bfloat16),
            pltpu.VMEM((3 * halo, cell_count), jnp.bfloat16),
            pltpu.VMEM((CHUNKS, chunk, 3 * cell_count), jnp.bfloat16),
            pltpu.VMEM((used, 2 * cell_count), jnp.bfloat16),
            pltpu.VMEM((2, CHUNKS, used, chunk), jnp.float32),
            pltpu.VMEM((2, CHUNKS, halo, chunk), jnp.float32),
            pltpu.SemaphoreType.DMA((fields_n,)),
            pltpu.SemaphoreType.DMA((2, CHUNKS, 6)),
            pltpu.SemaphoreType.DMA((2, CHUNKS, 6)),
        ],
        compiler_params=pltpu.CompilerParams(
            collective_id=0, has_side_effects=True, vmem_limit_bytes=44 * 1024 * 1024
        ),
        name="diffuse",
    )(field, near, coef, cols)
    second = second[: fields_n * stride].reshape(fields_n, stride, cell_count)[:, :levels_n]
    return -level_coef[None, :, None] * second


def solution(mesh):
    return jax.shard_map(
        functools.partial(shards, mesh.shape["cells"]),
        mesh=mesh,
        in_specs=(
            P(None, None, "cells"),
            P("cells"),
            P("cells"),
            P("cells"),
            P(None, "cells"),
            P(None, "cells"),
            P(None, "cells"),
            P(),
        ),
        out_specs=P(None, None, "cells"),
        check_vma=False,
    )
```

profile of v0, /device:TPU:0, one launch (start us, length us, event | category | flops | bytes accessed | tf_op | source)
XLA Modules:
  0.0 45.5 jit_solution(2256880559030441489)
XLA Ops:
  0.0 2.1 %prepare.1 = (s32[8,1024]{1,0:T(8,128)}, f32[8,1024]{1,0:T(8,128)}, s32[176,128]{1,0:T(8,128)}) custom-call(f32[3232]{0:T(1024)} %dv_hbm.1, f32[3232]{0:T(1024)} %dc_hbm.1, s32[2,3232]{1,0:T(2,128)} %ends_hbm.1, s32[6,1024]{1,0:T(8,128)} %edges_hbm.1, s32[6,64]{1,0:T(8,128)} %send_hbm.1, f32[1024]{0:T(1024)} %area_hbm.1), custom_call_target="tpu_custom_call" | custom-call | tf_op jit(solution)/shard_map/prepare/pallas_call | solution.py:261
  2.1 0.0 copy-start
  2.1 1.6 %copy-done = f32[9,55,1024]{2,1,0:T(8,128)S(1)} copy-done((f32[9,55,1024]{2,1,0:T(8,128)S(1)}, f32[9,55,1024]{2,1,0:T(8,128)}, u32[]{:S(2)}) %copy-start) | copy-done | bytes 2027544
  3.7 0.0 copy-start.1
  3.7 0.9 %copy-done.1 = s32[176,128]{1,0:T(8,128)S(1)} copy-done((s32[176,128]{1,0:T(8,128)S(1)}, s32[176,128]{1,0:T(8,128)}, u32[]{:S(2)}) %copy-start.1) | copy-done | bytes 90136
  4.6 0.0 copy-start.2
  4.6 0.8 %copy-done.2 = s32[8,1024]{1,0:T(8,128)S(1)} copy-done((s32[8,1024]{1,0:T(8,128)S(1)}, s32[8,1024]{1,0:T(8,128)}, u32[]{:S(2)}) %copy-start.2) | copy-done | bytes 32792
  5.3 0.0 copy-start.3
  5.3 0.8 %copy-done.3 = f32[8,1024]{1,0:T(8,128)S(1)} copy-done((f32[8,1024]{1,0:T(8,128)S(1)}, f32[8,1024]{1,0:T(8,128)}, u32[]{:S(2)}) %copy-start.3) | copy-done | bytes 32792
  6.1 37.2 %diffuse.1 = f32[512,1024]{1,0:T(8,128)S(1)} custom-call(f32[9,55,1024]{2,1,0:T(8,128)S(1)} %copy-done, s32[8,1024]{1,0:T(8,128)S(1)} %copy-done.2, f32[8,1024]{1,0:T(8,128)S(1)} %copy-done.3, s32[176,128]{1,0:T(8,128)S(1)} %copy-done.1), custom_call_target="tpu_custom_call" | custom-call | tf_op jit(solution)/shard_map/diffuse/pallas_call | solution.py:292
  43.3 0.0 copy-start.4
  43.3 0.1 slice.6
  43.5 0.5 %copy-done.4 = f32[55]{0:T(128)S(1)} copy-done((f32[55]{0:T(128)S(1)}, f32[55]{0:T(128)}, u32[]{:S(2)}) %copy-start.4) | copy-done | bytes 244
  44.0 1.6 %slice_multiply_fusion = f32[9,55,1024]{2,1,0:T(8,128)} fusion(f32[9,56,1024]{2,1,0:T(8,128)S(1)} %bitcast.1, f32[55]{0:T(128)S(1)} %neg.4), kind=kLoop, calls=%fused_computation | loop fusion | flops 506880 | bytes 4055260 | tf_op jit(solution)/shard_map/mul | solution.py:317
  (1 shorter events, 0.0 us)
Async XLA Ops:
  2.1 1.6 %copy-start = (f32[9,55,1024]{2,1,0:T(8,128)S(1)}, f32[9,55,1024]{2,1,0:T(8,128)}, u32[]{:S(2)}) copy-start(f32[9,55,1024]{2,1,0:T(8,128)} %field_ref.1) | copy-start | bytes 6082564
  3.7 0.9 %copy-start.1 = (s32[176,128]{1,0:T(8,128)S(1)}, s32[176,128]{1,0:T(8,128)}, u32[]{:S(2)}) copy-start(s32[176,128]{1,0:T(8,128)} %get-tuple-element.10.cols_ref) | copy-start | bytes 270340
  4.6 0.8 %copy-start.2 = (s32[8,1024]{1,0:T(8,128)S(1)}, s32[8,1024]{1,0:T(8,128)}, u32[]{:S(2)}) copy-start(s32[8,1024]{1,0:T(8,128)} %get-tuple-element.8.near_ref) | copy-start | bytes 98308
  5.3 0.8 %copy-start.3 = (f32[8,1024]{1,0:T(8,128)S(1)}, f32[8,1024]{1,0:T(8,128)}, u32[]{:S(2)}) copy-start(f32[8,1024]{1,0:T(8,128)} %get-tuple-element.9.coef_ref) | copy-start | bytes 98308
  43.3 0.7 %copy-start.4 = (f32[55]{0:T(128)S(1)}, f32[55]{0:T(128)}, u32[]{:S(2)}) copy-start(f32[55]{0:T(128)} %param.15) | copy-start | bytes 664
where the time goes:
time: 45.9 us; the launch traced here: 45.5 us
  Pallas kernels  39.3 us (86%)
  local copies, waits for them, and re-layouts  4.62 us (10%)
  other arithmetic  1.56 us (3%)
    pallas_call x1, Pallas kernels, shards(): pl.pallas_call(functools.partial(main_kernel, devices, length), out_shape...  37.2 us
    unnamed x10, local copies, waits for them, and re-layouts  4.49 us
    pallas_call x1, Pallas kernels, shards(): pl.pallas_call(prepare_kernel, out_shape=(jax.ShapeDtypeStruct((8, cell_c...  2.09 us
    mul x1, other arithmetic, shards(): return -level_coef[None, :, None] * second  1.56 us

commit v1 on v0

v1 whole, which is shorter than its diff:
```python
import functools

import jax
import jax.numpy as jnp
from jax import lax
from jax.experimental import pallas as pl
from jax.experimental.pallas import tpu as pltpu
from jax.sharding import PartitionSpec as P

CELLS_Y = 16
BLOCK_ROW = 16
OFFSETS = (1, -1, BLOCK_ROW, -BLOCK_ROW, BLOCK_ROW - 1, 1 - BLOCK_ROW)
LANES = 128
CUTS = (1, 1, 1, 1)


def up(value, step):
    return -(-value // step) * step


def slots(length):
    side = CELLS_Y
    counts = (side, side, length, length, 1, 1)
    order = (2, 3, 0, 1, 4, 5)
    base = [0] * 6
    at = 0
    for k in order:
        base[k] = at
        at += up(counts[k], 8)
    return tuple(base), counts, at


def bounds(rows):
    parts = rows // LANES
    total = sum(CUTS)
    edges = [0]
    for k in range(len(CUTS)):
        edges.append(parts * sum(CUTS[: k + 1]) // total * LANES)
    return edges


def split(values):
    high = values.astype(jnp.bfloat16)
    low = (values - high.astype(jnp.float32)).astype(jnp.bfloat16)
    return high, low


def kernel(
    devices,
    field_hbm, dv_hbm, dc_hbm, ends_hbm, edges_hbm, send_hbm, area_hbm, level_hbm,
    out_ref,
    landed, flat, first, matrix, rim, pair, selector, outgoing, incoming, corner_out, corner_in,
    weight, packed, index, near_ref, coef_ref,
    dv_ref, dc_ref, ends_ref, edges_ref, send_ref, area_ref, level_ref, scale_ref,
    load_sem, table_sem, send_sem, recv_sem,
):
    fields_n, levels_n, cell_count = field_hbm.shape
    stride = up(levels_n, 8)
    rows = flat.shape[0]
    cuts = bounds(rows)
    chunks = len(cuts) - 1
    halo = rim.shape[0] // 2
    length = send_ref.shape[1]
    edge_count = ends_ref.shape[1]
    base, counts, used = slots(length)
    me = lax.axis_index("cells")
    targets = [lax.rem(me + (o + devices), devices) for o in OFFSETS]
    tiles = cell_count // LANES

    send_load = pltpu.make_async_copy(send_hbm, send_ref, table_sem.at[0])
    send_load.start()
    loads = [
        pltpu.make_async_copy(field_hbm.at[f], landed.at[f], load_sem.at[f])
        for f in range(fields_n)
    ]
    for load in loads:
        load.start()
    pairs = (
        (dv_hbm, dv_ref), (dc_hbm, dc_ref), (ends_hbm, ends_ref), (edges_hbm, edges_ref),
        (area_hbm, area_ref), (level_hbm, level_ref),
    )
    tables = [
        pltpu.make_async_copy(a, b, table_sem.at[i + 1]) for i, (a, b) in enumerate(pairs)
    ]
    for load in tables:
        load.start()

    barrier = pltpu.get_barrier_semaphore()
    for target in targets:
        pl.semaphore_signal(
            barrier, inc=1, device_id=(target,), device_id_type=pl.DeviceIdType.MESH
        )

    send_load.wait()
    for k in range(6):
        height = up(counts[k], 8)
        r = lax.broadcasted_iota(jnp.int32, (height, length), 0)
        c = lax.broadcasted_iota(jnp.int32, (height, length), 1)
        ids = send_ref[k : k + 1, :].astype(jnp.float32)
        column = jnp.sum(jnp.where(r == c, ids, 0.0), axis=1, keepdims=True)
        column = jnp.broadcast_to(column, (height, LANES)).astype(jnp.int32)
        lane = lax.broadcasted_iota(jnp.int32, (height, LANES), 1)
        for tile in range(tiles):
            hit = column == lane + tile * LANES
            ones = jnp.where(hit, 1.0, 0.0).astype(jnp.bfloat16)
            selector[base[k] : base[k] + height, tile * LANES : (tile + 1) * LANES] = ones

    def spread(values, c):
        low_at = cuts[c + 1] - cuts[c]
        high, low = split(values)
        pair[2 * cuts[c] : 2 * cuts[c] + low_at, :] = high
        pair[2 * cuts[c] + low_at : 2 * cuts[c + 1], :] = low

    def copies(lap, c):
        here = pl.ds(cuts[c], cuts[c + 1] - cuts[c])

        def ends(k):
            if k < 4:
                some = pl.ds(base[k], counts[k])
                return outgoing.at[lap, some, here], incoming.at[lap, some, here]
            return corner_out.at[lap, k - 4, :, here], corner_in.at[lap, k - 4, :, here]

        return [
            pltpu.make_async_remote_copy(
                src_ref=ends(k)[0],
                dst_ref=ends(k)[1],
                send_sem=send_sem.at[lap, c, k],
                recv_sem=recv_sem.at[lap, c, k],
                device_id=(targets[k],),
                device_id_type=pl.DeviceIdType.MESH,
            )
            for k in (2, 3, 4, 5, 0, 1)
        ]

    def send(lap, c):
        size = cuts[c + 1] - cuts[c]
        both = lax.dot_general(
            selector[...],
            pair[2 * cuts[c] : 2 * cuts[c + 1], :],
            (((1,), (1,)), ((), ())),
            preferred_element_type=jnp.float32,
        )
        here = slice(cuts[c], cuts[c + 1])
        both = both[:, :size] + both[:, size:]
        outgoing[lap, :, here] = both[: base[4]]
        for k in (4, 5):
            corner_out[lap, k - 4, :, here] = both[base[k] : base[k] + 1]
        for copy in copies(lap, c):
            copy.start()

    def own(c):
        size = cuts[c + 1] - cuts[c]
        at = 2 * cuts[c]
        both = jnp.dot(
            pair[at : at + 2 * size, :],
            matrix[:cell_count, :],
            preferred_element_type=jnp.float32,
        )
        fine = jnp.dot(
            pair[at : at + size, :],
            matrix[cell_count:, :],
            preferred_element_type=jnp.float32,
        )
        return both[:size] + both[size:] + fine

    def outside(lap, c):
        size = cuts[c + 1] - cuts[c]
        here = slice(cuts[c], cuts[c + 1])
        for copy in copies(lap, c):
            copy.wait_recv()
        corners = jnp.zeros((halo - base[4], size), jnp.float32)
        place = lax.broadcasted_iota(jnp.int32, corners.shape, 0)
        for k in (4, 5):
            value = jnp.broadcast_to(corner_in[lap, k - 4, :, here], corners.shape)
            corners = jnp.where(place == base[k] - base[4], value, corners)
        whole = jnp.concatenate([incoming[lap, :, here], corners], axis=0)
        high, low = split(whole.T)
        lhs = jnp.concatenate([high, low], axis=0)
        both = jnp.dot(lhs, rim[:halo, :], preferred_element_type=jnp.float32)
        fine = jnp.dot(high, rim[halo:, :], preferred_element_type=jnp.float32)
        return both[:size] + both[size:] + fine

    loaded = 0
    for c in range(chunks):
        need = min(fields_n, -(-cuts[c + 1] // stride))
        for f in range(loaded, need):
            loads[f].wait()
            flat[f * stride : f * stride + levels_n, :] = landed[f]
        loaded = max(loaded, need)
        spread(flat[cuts[c] : cuts[c + 1], :], c)
        if c == 0:
            pl.semaphore_wait(barrier, len(targets))
        send(0, c)

    for load in tables:
        load.wait()
    edge_tiles = weight.shape[1] // LANES
    weight[...] = jnp.zeros_like(weight)
    packed[...] = jnp.zeros_like(packed)
    index[...] = jnp.zeros_like(index)
    for k in range(edge_tiles):
        part = slice(k * LANES, min((k + 1) * LANES, edge_count))
        weight[0, part] = dv_ref[part] / dc_ref[part]
    packed[:, :edge_count] = ends_ref[0:1, :] + ends_ref[1:2, :] * 4096
    index[0:6, :] = edges_ref[...]
    row = lax.broadcasted_iota(jnp.int32, (8, LANES), 0)
    lane = lax.broadcasted_iota(jnp.int32, (8, LANES), 1)
    for tile in range(tiles):
        here = slice(tile * LANES, (tile + 1) * LANES)
        wanted = index[:, here]
        high = wanted >> 7
        low = wanted & 127
        w = jnp.zeros((8, LANES), jnp.float32)
        p = jnp.zeros((8, LANES), jnp.int32)
        for k in range(edge_tiles):
            part = slice(k * LANES, (k + 1) * LANES)
            wk = jnp.broadcast_to(weight[0:1, part], (8, LANES))
            pk = jnp.broadcast_to(packed[0:1, part], (8, LANES))
            hit = high == k
            w = jnp.where(hit, jnp.take_along_axis(wk, low, axis=1), w)
            p = jnp.where(hit, jnp.take_along_axis(pk, low, axis=1), p)
        lower = p & 4095
        upper = p >> 12
        other = jnp.where(lower == lane + tile * LANES, upper, lower)
        away = other - cell_count
        place = jnp.zeros((8, LANES), jnp.int32)
        for k in range(6):
            inside = (away >= k * length) & (away < (k + 1) * length)
            place = jnp.where(inside, away - k * length + base[k], place)
        near = jnp.where(away < 0, other, cell_count + place)
        share = w / jnp.broadcast_to(area_ref[here], (8, LANES))
        share = jnp.where(row < 6, share, 0.0)
        total = jnp.sum(share, axis=0, keepdims=True)
        near_ref[:, here] = jnp.where(row < 6, near, -1)
        coef_ref[:, here] = jnp.where(row == 6, total, share)
    r = lax.broadcasted_iota(jnp.int32, (stride, levels_n), 0)
    c = lax.broadcasted_iota(jnp.int32, (stride, levels_n), 1)
    levels = jnp.broadcast_to(level_ref[...].reshape(1, levels_n), (stride, levels_n))
    column = jnp.sum(jnp.where(r == c, -levels, 0.0), axis=1, keepdims=True)
    scale_ref[...] = jnp.broadcast_to(column, (stride, LANES))

    ids = lax.broadcasted_iota(jnp.int32, (LANES, LANES), 0)

    def entries(start, tile):
        here = slice(tile * LANES, (tile + 1) * LANES)
        block = jnp.zeros((LANES, LANES), jnp.float32)
        for j in range(6):
            hit = ids == near_ref[j : j + 1, here] - start
            block = jnp.where(hit, coef_ref[j : j + 1, here], block)
        return split(block)

    def fill(r, carry):
        start = pl.multiple_of(r * LANES, LANES)
        for tile in range(tiles):
            here = slice(tile * LANES, (tile + 1) * LANES)
            high, low = entries(start, tile)
            matrix[pl.ds(start, LANES), here] = high
            matrix[pl.ds(start + cell_count, LANES), here] = low
        return carry

    lax.fori_loop(0, tiles, fill, 0)
    for r in range(halo // LANES):
        for tile in range(tiles):
            here = slice(tile * LANES, (tile + 1) * LANES)
            high, low = entries(cell_count + r * LANES, tile)
            rim[r * LANES : (r + 1) * LANES, here] = high
            rim[halo + r * LANES : halo + (r + 1) * LANES, here] = low

    for c in range(chunks):
        part = slice(cuts[c], cuts[c + 1])
        first[part, :] = own(c) - flat[part, :] * coef_ref[6:7, :]
        result = first[part, :] + outside(0, c)
        first[part, :] = result
        spread(result, c)
        send(1, c)
    for c in range(chunks):
        part = slice(cuts[c], cuts[c + 1])
        flat[part, :] = own(c) - first[part, :] * coef_ref[6:7, :]
    for c in range(chunks):
        part = slice(cuts[c], cuts[c + 1])
        flat[part, :] = flat[part, :] + outside(1, c)
        for f in range(fields_n):
            lo = max(cuts[c], f * stride)
            hi = min(cuts[c + 1], (f + 1) * stride)
            if lo >= hi:
                continue
            at = lo - f * stride
            size = min(hi - f * stride, levels_n) - at
            scale = jnp.broadcast_to(scale_ref[at : at + size, 0:1], (size, cell_count))
            out_ref[f, at : at + size, :] = flat[lo : lo + size, :] * scale
    for lap in range(2):
        for c in range(chunks):
            for copy in copies(lap, c):
                copy.wait_send()


def shards(
    devices, field, cell_area, dv_edge, dc_edge, cells_on_edge, edges_on_cell, send_cells,
    level_coef,
):
    length = send_cells.shape[1]
    fields_n, levels_n, cell_count = field.shape
    edge_count = dv_edge.shape[0]
    base, _, used = slots(length)
    halo = up(used, LANES)
    stride = up(levels_n, 8)
    rows = up(fields_n * stride, LANES)
    chunks = len(bounds(rows)) - 1
    vmem = pl.BlockSpec(memory_space=pltpu.VMEM)
    hbm = pl.BlockSpec(memory_space=pltpu.HBM)
    return pl.pallas_call(
        functools.partial(kernel, devices),
        out_shape=pltpu.VMEM(field.shape, jnp.float32),
        in_specs=[hbm] * 8,
        out_specs=vmem,
        scratch_shapes=[
            pltpu.VMEM(field.shape, jnp.float32),
            pltpu.VMEM((rows, cell_count), jnp.float32),
            pltpu.VMEM((rows, cell_count), jnp.float32),
            pltpu.VMEM((2 * cell_count, cell_count), jnp.bfloat16),
            pltpu.VMEM((2 * halo, cell_count), jnp.bfloat16),
            pltpu.VMEM((2 * rows, cell_count), jnp.bfloat16),
            pltpu.VMEM((used, cell_count), jnp.bfloat16),
            pltpu.VMEM((2, base[4], rows), jnp.float32),
            pltpu.VMEM((2, base[4], rows), jnp.float32),
            pltpu.VMEM((2, 2, 1, rows), jnp.float32),
            pltpu.VMEM((2, 2, 1, rows), jnp.float32),
            pltpu.VMEM((1, up(edge_count, LANES)), jnp.float32),
            pltpu.VMEM((1, up(edge_count, LANES)), jnp.int32),
            pltpu.VMEM((8, cell_count), jnp.int32),
            pltpu.VMEM((8, cell_count), jnp.int32),
            pltpu.VMEM((8, cell_count), jnp.float32),
            pltpu.VMEM(dv_edge.shape, jnp.float32),
            pltpu.VMEM(dc_edge.shape, jnp.float32),
            pltpu.VMEM(cells_on_edge.shape, jnp.int32),
            pltpu.VMEM(edges_on_cell.shape, jnp.int32),
            pltpu.VMEM(send_cells.shape, jnp.int32),
            pltpu.VMEM(cell_area.shape, jnp.float32),
            pltpu.VMEM(level_coef.shape, jnp.float32),
            pltpu.VMEM((stride, LANES), jnp.float32),
            pltpu.SemaphoreType.DMA((fields_n,)),
            pltpu.SemaphoreType.DMA((7,)),
            pltpu.SemaphoreType.DMA((2, chunks, 6)),
            pltpu.SemaphoreType.DMA((2, chunks, 6)),
        ],
        compiler_params=pltpu.CompilerParams(
            collective_id=0,
            has_side_effects=True,
            vmem_limit_bytes=67043328 - up(fields_n * stride * cell_count * 4, 1024),
        ),
        name="diffuse",
    )(
        field, dv_edge, dc_edge, cells_on_edge, edges_on_cell, send_cells, cell_area, level_coef
    )


def solution(mesh):
    return jax.shard_map(
        functools.partial(shards, mesh.shape["cells"]),
        mesh=mesh,
        in_specs=(
            P(None, None, "cells"),
            P("cells"),
            P("cells"),
            P("cells"),
            P(None, "cells"),
            P(None, "cells"),
            P(None, "cells"),
            P(),
        ),
        out_specs=P(None, None, "cells"),
        check_vma=False,
    )
```

time: 45.9 us -> 33.4 us (0.73)
  Pallas kernels: 39.3 us -> 32 us
  local copies, waits for them, and re-layouts: 4.62 us -> 1.31 us
  other arithmetic: 1.56 us -> 0 us
    pallas_call x2 -> x1, Pallas kernels: 39.3 us -> 32 us  [shards(): pl.pallas_call(functools.partial(kernel, devices), out_shape=pltpu.VMEM(f...]
    unnamed x10 -> x1, local copies, waits for them, and re-layouts: 4.49 us -> 1.31 us
    mul x1 -> x0, other arithmetic: 1.56 us -> none  [shards(): return -level_coef[None, :, None] * second]
where the time goes in v1:
time: 33.4 us; the launch traced here: 33.3 us
  Pallas kernels  32 us (96%)
  local copies, waits for them, and re-layouts  1.31 us (4%)
    pallas_call x1, Pallas kernels, shards(): pl.pallas_call(functools.partial(kernel, devices), out_shape=pltpu.VMEM(f...  32 us
    unnamed x1, local copies, waits for them, and re-layouts  1.31 us

profile of v1, /device:TPU:0, one launch (start us, length us, event | category | flops | bytes accessed | tf_op | source)
XLA Modules:
  0.0 33.3 jit_solution(18435110895071438372)
XLA Ops:
  0.0 32.0 %diffuse.1 = f32[9,55,1024]{2,1,0:T(8,128)S(1)} custom-call(f32[9,55,1024]{2,1,0:T(8,128)} %field_hbm.1, f32[3232]{0:T(1024)} %dv_hbm.1, f32[3232]{0:T(1024)} %dc_hbm.1, s32[2,3232]{1,0:T(2,128)} %ends_hbm.1, s32[6,1024]{1,0:T(8,128)} %edges_hbm.1, s32[6,64]{1,0:T(8,128)} %send_hbm.1, f32[1024]{0:T(1024)} %area_hbm.1, f32[55]{0:T(128)} %level_hbm.1), custom_call_target="tpu_custom_call" | custom-call | tf_op jit(solution)/shard_map/diffuse/pallas_call | solution.py:311
  32.0 1.3 %copy.10 = f32[9,55,1024]{2,1,0:T(8,128)} copy(f32[9,55,1024]{2,1,0:T(8,128)S(1)} %diffuse.1) | data formatting | bytes 4055040

commit v2 on v1

--- a/solution.py
+++ b/solution.py
@@ -11,7 +11,9 @@
 BLOCK_ROW = 16
 OFFSETS = (1, -1, BLOCK_ROW, -BLOCK_ROW, BLOCK_ROW - 1, 1 - BLOCK_ROW)
 LANES = 128
-CUTS = (1, 1, 1, 1)
+UNIT = 16
+CUTS = (8, 8, 8, 7)
+ORDER = ((1, 0), (1, 1), (1, 2), (1, 3), (0, 0), (0, 1), (0, 2), (0, 3), (2, 0), (2, 1), (2, 2), (2, 3))
 
 
 def up(value, step):
@@ -26,17 +28,32 @@
     at = 0
     for k in order:
         base[k] = at
-        at += up(counts[k], 8)
+        at += counts[k]
     return tuple(base), counts, at
 
 
+def layout(fields_n, levels_n):
+    stride = up(levels_n, 8)
+    whole = levels_n // 8 * 8
+    rest = levels_n - whole
+    gaps = [
+        f * stride + l for f in range(fields_n - 1) for l in range(levels_n, stride)
+    ]
+    last = (fields_n - 1) * stride
+    parts = [(f, 0, levels_n, f * stride) for f in range(fields_n - 1)]
+    if rest <= len(gaps) and (last + whole) % UNIT == 0:
+        parts.append((fields_n - 1, 0, whole, last))
+        parts += [(fields_n - 1, whole + i, 1, gaps[i]) for i in range(rest)]
+        return parts, gaps[rest:], last + whole
+    parts.append((fields_n - 1, 0, levels_n, last))
+    rows = up(last + levels_n, UNIT)
+    return parts, gaps + list(range(last + levels_n, rows)), rows
+
+
 def bounds(rows):
-    parts = rows // LANES
+    parts = rows // UNIT
     total = sum(CUTS)
-    edges = [0]
-    for k in range(len(CUTS)):
-        edges.append(parts * sum(CUTS[: k + 1]) // total * LANES)
-    return edges
+    return [parts * sum(CUTS[:k]) // total * UNIT for k in range(len(CUTS) + 1)]
 
 
 def split(values):
@@ -49,16 +66,17 @@
     devices,
     field_hbm, dv_hbm, dc_hbm, ends_hbm, edges_hbm, send_hbm, area_hbm, level_hbm,
     out_ref,
-    landed, flat, first, matrix, rim, pair, selector, outgoing, incoming, corner_out, corner_in,
-    weight, packed, index, near_ref, coef_ref,
+    landed, flat, first, matrix, rim, pair, selector, rim_out, rim_in, side_out, side_in,
+    corner_out, corner_in, lists, weight, packed, index, near_ref, coef_ref,
     dv_ref, dc_ref, ends_ref, edges_ref, send_ref, area_ref, level_ref, scale_ref,
     load_sem, table_sem, send_sem, recv_sem,
 ):
     fields_n, levels_n, cell_count = field_hbm.shape
-    stride = up(levels_n, 8)
-    rows = flat.shape[0]
+    parts, gaps, rows = layout(fields_n, levels_n)
     cuts = bounds(rows)
     chunks = len(cuts) - 1
+    widths = [up(cuts[c + 1] - cuts[c], LANES) for c in range(chunks)]
+    starts = [sum(widths[:c]) for c in range(chunks)]
     halo = rim.shape[0] // 2
     length = send_ref.shape[1]
     edge_count = ends_ref.shape[1]
@@ -66,6 +84,12 @@
     me = lax.axis_index("cells")
     targets = [lax.rem(me + (o + devices), devices) for o in OFFSETS]
     tiles = cell_count // LANES
+
+    barrier = pltpu.get_barrier_semaphore()
+    for target in targets:
+        pl.semaphore_signal(
+            barrier, inc=1, device_id=(target,), device_id_type=pl.DeviceIdType.MESH
+        )
 
     send_load = pltpu.make_async_copy(send_hbm, send_ref, table_sem.at[0])
     send_load.start()
@@ -85,25 +109,23 @@
     for load in tables:
         load.start()
 
-    barrier = pltpu.get_barrier_semaphore()
-    for target in targets:
-        pl.semaphore_signal(
-            barrier, inc=1, device_id=(target,), device_id_type=pl.DeviceIdType.MESH
-        )
-
     send_load.wait()
+    lists[0:6, 0:length] = send_ref[...]
+    table = lists[...]
+    lane = lax.broadcasted_iota(jnp.int32, (1, LANES), 1)
+    picks = [jnp.full((1, LANES), -1, jnp.int32)] * (halo // LANES)
     for k in range(6):
-        height = up(counts[k], 8)
-        r = lax.broadcasted_iota(jnp.int32, (height, length), 0)
-        c = lax.broadcasted_iota(jnp.int32, (height, length), 1)
-        ids = send_ref[k : k + 1, :].astype(jnp.float32)
-        column = jnp.sum(jnp.where(r == c, ids, 0.0), axis=1, keepdims=True)
-        column = jnp.broadcast_to(column, (height, LANES)).astype(jnp.int32)
-        lane = lax.broadcasted_iota(jnp.int32, (height, LANES), 1)
-        for tile in range(tiles):
-            hit = column == lane + tile * LANES
-            ones = jnp.where(hit, 1.0, 0.0).astype(jnp.bfloat16)
-            selector[base[k] : base[k] + height, tile * LANES : (tile + 1) * LANES] = ones
+        tile, at = base[k] // LANES, base[k] % LANES
+        moved = pltpu.roll(table, at, 1) if at else table
+        inside = (lane >= at) & (lane < at + counts[k])
+        picks[tile] = jnp.where(inside, moved[k : k + 1], picks[tile])
+    ids = lax.broadcasted_iota(jnp.int32, (LANES, LANES), 0)
+    for r in range(tiles):
+        for tile in range(halo // LANES):
+            hit = ids == picks[tile] - r * LANES
+            selector[r * LANES : (r + 1) * LANES, tile * LANES : (tile + 1) * LANES] = (
+                jnp.where(hit, 1.0, 0.0).astype(jnp.bfloat16)
+            )
 
     def spread(values, c):
         low_at = cuts[c + 1] - cuts[c]
@@ -112,12 +134,14 @@
         pair[2 * cuts[c] + low_at : 2 * cuts[c + 1], :] = low
 
     def copies(lap, c):
-        here = pl.ds(cuts[c], cuts[c + 1] - cuts[c])
+        half = pl.ds(cuts[c] // 2, (cuts[c + 1] - cuts[c]) // 2)
+        here = pl.ds(starts[c], widths[c])
 
         def ends(k):
-            if k < 4:
-                some = pl.ds(base[k], counts[k])
-                return outgoing.at[lap, some, here], incoming.at[lap, some, here]
+            if k in (2, 3):
+                return rim_out.at[lap, k - 2, half], rim_in.at[lap, k - 2, half]
+            if k in (0, 1):
+                return side_out.at[lap, k, :, here], side_in.at[lap, k, :, here]
             return corner_out.at[lap, k - 4, :, here], corner_in.at[lap, k - 4, :, here]
 
         return [
@@ -129,22 +153,36 @@
                 device_id=(targets[k],),
                 device_id_type=pl.DeviceIdType.MESH,
             )
-            for k in (2, 3, 4, 5, 0, 1)
+            for k in (4, 5, 0, 1, 2, 3)
         ]
 
     def send(lap, c):
         size = cuts[c + 1] - cuts[c]
-        both = lax.dot_general(
+        h = size // 2
+        both = jnp.dot(
+            pair[2 * cuts[c] : 2 * cuts[c + 1], :],
             selector[...],
-            pair[2 * cuts[c] : 2 * cuts[c + 1], :],
-            (((1,), (1,)), ((), ())),
             preferred_element_type=jnp.float32,
         )
-        here = slice(cuts[c], cuts[c + 1])
-        both = both[:, :size] + both[:, size:]
-        outgoing[lap, :, here] = both[: base[4]]
+        both = both[:size] + both[size:]
+        edge = both[:, :LANES]
+        turned = pltpu.roll(edge, length, 1)
+        left = lax.broadcasted_iota(jnp.int32, (h, LANES), 1) < length
+        half = slice(cuts[c] // 2, cuts[c + 1] // 2)
+        rim_out[lap, 0, half, :] = jnp.where(left, edge[:h], turned[h:])
+        rim_out[lap, 1, half, :] = jnp.where(left, turned[:h], edge[h:])
+        small = both[:, LANES:]
+        if size < widths[c]:
+            fill = jnp.zeros((widths[c] - size, LANES), jnp.float32)
+            small = jnp.concatenate([small, fill], axis=0)
+        small = small.T
+        here = slice(starts[c], starts[c] + widths[c])
+        for k in (0, 1):
+            at = base[k] - LANES
+            side_out[lap, k, :, here] = small[at : at + counts[k]]
         for k in (4, 5):
-            corner_out[lap, k - 4, :, here] = both[base[k] : base[k] + 1]
+            at = base[k] - LANES
+            corner_out[lap, k - 4, :, here] = small[at : at + 1]
         for copy in copies(lap, c):
             copy.start()
 
@@ -165,28 +203,47 @@
 
     def outside(lap, c):
         size = cuts[c + 1] - cuts[c]
-        here = slice(cuts[c], cuts[c + 1])
+        h = size // 2
         for copy in copies(lap, c):
             copy.wait_recv()
-        corners = jnp.zeros((halo - base[4], size), jnp.float32)
+        half = slice(cuts[c] // 2, cuts[c + 1] // 2)
+        here = slice(starts[c], starts[c] + widths[c])
+        left = lax.broadcasted_iota(jnp.int32, (h, LANES), 1) < length
+        above = rim_in[lap, 0, half, :]
+        below = rim_in[lap, 1, half, :]
+        edge = jnp.concatenate(
+            [
+                jnp.where(left, above, pltpu.roll(below, length, 1)),
+                jnp.where(left, pltpu.roll(above, length, 1), below),
+            ],
+            axis=0,
+        )
+        ends = base[4] - LANES
+        corners = jnp.zeros((LANES - ends, widths[c]), jnp.float32)
         place = lax.broadcasted_iota(jnp.int32, corners.shape, 0)
         for k in (4, 5):
             value = jnp.broadcast_to(corner_in[lap, k - 4, :, here], corners.shape)
             corners = jnp.where(place == base[k] - base[4], value, corners)
-        whole = jnp.concatenate([incoming[lap, :, here], corners], axis=0)
-        high, low = split(whole.T)
+        small = jnp.concatenate(
+            [side_in[lap, 0, :, here], side_in[lap, 1, :, here], corners], axis=0
+        )
+        high, low = split(jnp.concatenate([edge, small.T[:size]], axis=1))
         lhs = jnp.concatenate([high, low], axis=0)
         both = jnp.dot(lhs, rim[:halo, :], preferred_element_type=jnp.float32)
         fine = jnp.dot(high, rim[halo:, :], preferred_element_type=jnp.float32)
         return both[:size] + both[size:] + fine
 
-    loaded = 0
+    for row in gaps:
+        flat[row : row + 1, :] = jnp.zeros((1, cell_count), jnp.float32)
+    loaded = set()
     for c in range(chunks):
-        need = min(fields_n, -(-cuts[c + 1] // stride))
-        for f in range(loaded, need):
+        need = {f for f, _, _, row in parts if row < cuts[c + 1]}
+        for f in sorted(need - loaded):
             loads[f].wait()
-            flat[f * stride : f * stride + levels_n, :] = landed[f]
-        loaded = max(loaded, need)
+            for g, level, size, row in parts:
+                if g == f:
+                    flat[row : row + size, :] = landed[f, level : level + size, :]
+        loaded |= need
         spread(flat[cuts[c] : cuts[c + 1], :], c)
         if c == 0:
             pl.semaphore_wait(barrier, len(targets))
@@ -233,13 +290,12 @@
         total = jnp.sum(share, axis=0, keepdims=True)
         near_ref[:, here] = jnp.where(row < 6, near, -1)
         coef_ref[:, here] = jnp.where(row == 6, total, share)
-    r = lax.broadcasted_iota(jnp.int32, (stride, levels_n), 0)
-    c = lax.broadcasted_iota(jnp.int32, (stride, levels_n), 1)
-    levels = jnp.broadcast_to(level_ref[...].reshape(1, levels_n), (stride, levels_n))
+    tall = scale_ref.shape[0]
+    r = lax.broadcasted_iota(jnp.int32, (tall, levels_n), 0)
+    c = lax.broadcasted_iota(jnp.int32, (tall, levels_n), 1)
+    levels = jnp.broadcast_to(level_ref[...].reshape(1, levels_n), (tall, levels_n))
     column = jnp.sum(jnp.where(r == c, -levels, 0.0), axis=1, keepdims=True)
-    scale_ref[...] = jnp.broadcast_to(column, (stride, LANES))
-
-    ids = lax.broadcasted_iota(jnp.int32, (LANES, LANES), 0)
+    scale_ref[...] = jnp.broadcast_to(column, (tall, LANES))
 
     def entries(start, tile):
         here = slice(tile * LANES, (tile + 1) * LANES)
@@ -266,28 +322,32 @@
             rim[r * LANES : (r + 1) * LANES, here] = high
             rim[halo + r * LANES : halo + (r + 1) * LANES, here] = low
 
-    for c in range(chunks):
+    def relay(c):
         part = slice(cuts[c], cuts[c + 1])
         first[part, :] = own(c) - flat[part, :] * coef_ref[6:7, :]
         result = first[part, :] + outside(0, c)
         first[part, :] = result
         spread(result, c)
         send(1, c)
-    for c in range(chunks):
+
+    def inner(c):
         part = slice(cuts[c], cuts[c + 1])
         flat[part, :] = own(c) - first[part, :] * coef_ref[6:7, :]
-    for c in range(chunks):
+
+    def finish(c):
         part = slice(cuts[c], cuts[c + 1])
         flat[part, :] = flat[part, :] + outside(1, c)
-        for f in range(fields_n):
-            lo = max(cuts[c], f * stride)
-            hi = min(cuts[c + 1], (f + 1) * stride)
+        for f, level, size, row in parts:
+            lo = max(cuts[c], row)
+            hi = min(cuts[c + 1], row + size)
             if lo >= hi:
                 continue
-            at = lo - f * stride
-            size = min(hi - f * stride, levels_n) - at
-            scale = jnp.broadcast_to(scale_ref[at : at + size, 0:1], (size, cell_count))
-            out_ref[f, at : at + size, :] = flat[lo : lo + size, :] * scale
+            at = level + lo - row
+            scale = jnp.broadcast_to(scale_ref[at : at + hi - lo, 0:1], (hi - lo, cell_count))
+            out_ref[f, at : at + hi - lo, :] = flat[lo:hi, :] * scale
+
+    for step, c in ORDER:
+        (inner, relay, finish)[step](c)
     for lap in range(2):
         for c in range(chunks):
             for copy in copies(lap, c):
@@ -301,11 +361,12 @@
     length = send_cells.shape[1]
     fields_n, levels_n, cell_count = field.shape
     edge_count = dv_edge.shape[0]
-    base, _, used = slots(length)
+    _, _, used = slots(length)
     halo = up(used, LANES)
-    stride = up(levels_n, 8)
-    rows = up(fields_n * stride, LANES)
-    chunks = len(bounds(rows)) - 1
+    _, _, rows = layout(fields_n, levels_n)
+    cuts = bounds(rows)
+    chunks = len(cuts) - 1
+    wide = sum(up(cuts[c + 1] - cuts[c], LANES) for c in range(chunks))
     vmem = pl.BlockSpec(memory_space=pltpu.VMEM)
     hbm = pl.BlockSpec(memory_space=pltpu.HBM)
     return pl.pallas_call(
@@ -320,11 +381,14 @@
             pltpu.VMEM((2 * cell_count, cell_count), jnp.bfloat16),
             pltpu.VMEM((2 * halo, cell_count), jnp.bfloat16),
             pltpu.VMEM((2 * rows, cell_count), jnp.bfloat16),
-            pltpu.VMEM((used, cell_count), jnp.bfloat16),
-            pltpu.VMEM((2, base[4], rows), jnp.float32),
-            pltpu.VMEM((2, base[4], rows), jnp.float32),
-            pltpu.VMEM((2, 2, 1, rows), jnp.float32),
-            pltpu.VMEM((2, 2, 1, rows), jnp.float32),
+            pltpu.VMEM((cell_count, halo), jnp.bfloat16),
+            pltpu.VMEM((2, 2, rows // 2, 2 * length), jnp.float32),
+            pltpu.VMEM((2, 2, rows // 2, 2 * length), jnp.float32),
+            pltpu.VMEM((2, 2, CELLS_Y, wide), jnp.float32),
+            pltpu.VMEM((2, 2, CELLS_Y, wide), jnp.float32),
+            pltpu.VMEM((2, 2, 1, wide), jnp.float32),
+            pltpu.VMEM((2, 2, 1, wide), jnp.float32),
+            pltpu.VMEM((8, LANES), jnp.int32),
             pltpu.VMEM((1, up(edge_count, LANES)), jnp.float32),
             pltpu.VMEM((1, up(edge_count, LANES)), jnp.int32),
             pltpu.VMEM((8, cell_count), jnp.int32),
@@ -337,7 +401,7 @@
             pltpu.VMEM(send_cells.shape, jnp.int32),
             pltpu.VMEM(cell_area.shape, jnp.float32),
             pltpu.VMEM(level_coef.shape, jnp.float32),
-            pltpu.VMEM((stride, LANES), jnp.float32),
+            pltpu.VMEM((up(levels_n, 8), LANES), jnp.float32),
             pltpu.SemaphoreType.DMA((fields_n,)),
             pltpu.SemaphoreType.DMA((7,)),
             pltpu.SemaphoreType.DMA((2, chunks, 6)),
@@ -346,7 +410,7 @@
         compiler_params=pltpu.CompilerParams(
             collective_id=0,
             has_side_effects=True,
-            vmem_limit_bytes=67043328 - up(fields_n * stride * cell_count * 4, 1024),
+            vmem_limit_bytes=67043328 - fields_n * up(levels_n, 8) * cell_count * 4,
         ),
         name="diffuse",
     )(

time: 33.4 us -> 31.8 us (0.952)
  Pallas kernels: 32 us -> 30.1 us
    pallas_call x1, Pallas kernels: 32 us -> 30.1 us  [shards(): pl.pallas_call(functools.partial(kernel, devices), out_shape=pltpu.VMEM(f...]
where the time goes in v2:
time: 31.8 us; the launch traced here: 31.4 us
  Pallas kernels  30.1 us (95%)
  local copies, waits for them, and re-layouts  1.31 us (4%)
    pallas_call x1, Pallas kernels, shards(): pl.pallas_call(functools.partial(kernel, devices), out_shape=pltpu.VMEM(f...  30.1 us
    unnamed x1, local copies, waits for them, and re-layouts  1.31 us

profile of v2, /device:TPU:0, one launch (start us, length us, event | category | flops | bytes accessed | tf_op | source)
XLA Modules:
  0.0 31.4 jit_solution(6794473257177612076)
XLA Ops:
  0.0 30.1 %diffuse.1 = f32[9,55,1024]{2,1,0:T(8,128)S(1)} custom-call(f32[9,55,1024]{2,1,0:T(8,128)} %field_hbm.1, f32[3232]{0:T(1024)} %dv_hbm.1, f32[3232]{0:T(1024)} %dc_hbm.1, s32[2,3232]{1,0:T(2,128)} %ends_hbm.1, s32[6,1024]{1,0:T(8,128)} %edges_hbm.1, s32[6,64]{1,0:T(8,128)} %send_hbm.1, f32[1024]{0:T(1024)} %area_hbm.1, f32[55]{0:T(128)} %level_hbm.1), custom_call_target="tpu_custom_call" | custom-call | tf_op jit(solution)/shard_map/diffuse/pallas_call | solution.py:372
  30.1 1.3 %copy.10 = f32[9,55,1024]{2,1,0:T(8,128)} copy(f32[9,55,1024]{2,1,0:T(8,128)S(1)} %diffuse.1) | data formatting | bytes 4055040

commit v3 on v2

--- a/solution.py
+++ b/solution.py
@@ -56,6 +56,26 @@
     return [parts * sum(CUTS[:k]) // total * UNIT for k in range(len(CUTS) + 1)]
 
 
+def gather(parts, cuts):
+    groups = []
+    for f in range(1 + max(part[0] for part in parts)):
+        row = min(part[3] for part in parts if part[0] == f)
+        c = max(k for k in range(len(cuts)) if cuts[k] <= row)
+        if groups and groups[-1][2] == c:
+            groups[-1][1] += 1
+        else:
+            groups.append([f, 1, c])
+    return sorted(groups, key=lambda group: group[2])
+
+
+def strips(cuts):
+    starts = [0]
+    for c in range(len(cuts) - 1):
+        assert cuts[c + 1] - cuts[c] <= LANES
+        starts.append(starts[-1] + cuts[c + 1] - cuts[c] + 2 * CELLS_Y)
+    return starts
+
+
 def split(values):
     high = values.astype(jnp.bfloat16)
     low = (values - high.astype(jnp.float32)).astype(jnp.bfloat16)
@@ -66,7 +86,7 @@
     devices,
     field_hbm, dv_hbm, dc_hbm, ends_hbm, edges_hbm, send_hbm, area_hbm, level_hbm,
     out_ref,
-    landed, flat, first, matrix, rim, pair, selector, rim_out, rim_in, side_out, side_in,
+    landed, flat, first, matrix, rim, pair, selector, strip_out, strip_in,
     corner_out, corner_in, lists, weight, packed, index, near_ref, coef_ref,
     dv_ref, dc_ref, ends_ref, edges_ref, send_ref, area_ref, level_ref, scale_ref,
     load_sem, table_sem, send_sem, recv_sem,
@@ -75,8 +95,7 @@
     parts, gaps, rows = layout(fields_n, levels_n)
     cuts = bounds(rows)
     chunks = len(cuts) - 1
-    widths = [up(cuts[c + 1] - cuts[c], LANES) for c in range(chunks)]
-    starts = [sum(widths[:c]) for c in range(chunks)]
+    starts = strips(cuts)
     halo = rim.shape[0] // 2
     length = send_ref.shape[1]
     edge_count = ends_ref.shape[1]
@@ -93,9 +112,12 @@
 
     send_load = pltpu.make_async_copy(send_hbm, send_ref, table_sem.at[0])
     send_load.start()
+    groups = gather(parts, cuts)
     loads = [
-        pltpu.make_async_copy(field_hbm.at[f], landed.at[f], load_sem.at[f])
-        for f in range(fields_n)
+        pltpu.make_async_copy(
+            field_hbm.at[pl.ds(f, n)], landed.at[pl.ds(f, n)], load_sem.at[i]
+        )
+        for i, (f, n, _) in enumerate(groups)
     ]
     for load in loads:
         load.start()
@@ -133,28 +155,38 @@
         pair[2 * cuts[c] : 2 * cuts[c] + low_at, :] = high
         pair[2 * cuts[c] + low_at : 2 * cuts[c + 1], :] = low
 
+    def places(c):
+        h = (cuts[c + 1] - cuts[c]) // 2
+        at = starts[c]
+        side = at + 2 * h
+        return (
+            pl.ds(side, CELLS_Y), pl.ds(side + CELLS_Y, CELLS_Y), pl.ds(at, h), pl.ds(at + h, h)
+        )
+
     def copies(lap, c):
-        half = pl.ds(cuts[c] // 2, (cuts[c + 1] - cuts[c]) // 2)
-        here = pl.ds(starts[c], widths[c])
-
         def ends(k):
-            if k in (2, 3):
-                return rim_out.at[lap, k - 2, half], rim_in.at[lap, k - 2, half]
-            if k in (0, 1):
-                return side_out.at[lap, k, :, here], side_in.at[lap, k, :, here]
-            return corner_out.at[lap, k - 4, :, here], corner_in.at[lap, k - 4, :, here]
+            if k < 4:
+                here = places(c)[k]
+                return strip_out.at[lap, here], strip_in.at[lap, here]
+            return corner_out.at[lap, c, k - 4], corner_in.at[lap, c, k - 4]
 
         return [
             pltpu.make_async_remote_copy(
                 src_ref=ends(k)[0],
                 dst_ref=ends(k)[1],
-                send_sem=send_sem.at[lap, c, k],
-                recv_sem=recv_sem.at[lap, c, k],
+                send_sem=send_sem.at[k // 4],
+                recv_sem=recv_sem.at[lap, c, k // 4],
                 device_id=(targets[k],),
                 device_id_type=pl.DeviceIdType.MESH,
             )
             for k in (4, 5, 0, 1, 2, 3)
         ]
+
+    def receive(lap, c):
+        strip = strip_in.at[lap, pl.ds(starts[c], starts[c + 1] - starts[c])]
+        pltpu.make_async_copy(strip, strip, recv_sem.at[lap, c, 0]).wait()
+        corner = corner_in.at[lap, c]
+        pltpu.make_async_copy(corner, corner, recv_sem.at[lap, c, 1]).wait()
 
     def send(lap, c):
         size = cuts[c + 1] - cuts[c]
@@ -168,21 +200,20 @@
         edge = both[:, :LANES]
         turned = pltpu.roll(edge, length, 1)
         left = lax.broadcasted_iota(jnp.int32, (h, LANES), 1) < length
-        half = slice(cuts[c] // 2, cuts[c + 1] // 2)
-        rim_out[lap, 0, half, :] = jnp.where(left, edge[:h], turned[h:])
-        rim_out[lap, 1, half, :] = jnp.where(left, turned[:h], edge[h:])
+        where = places(c)
+        strip_out[lap, where[2], :] = jnp.where(left, edge[:h], turned[h:])
+        strip_out[lap, where[3], :] = jnp.where(left, turned[:h], edge[h:])
         small = both[:, LANES:]
-        if size < widths[c]:
-            fill = jnp.zeros((widths[c] - size, LANES), jnp.float32)
+        if size < LANES:
+            fill = jnp.zeros((LANES - size, LANES), jnp.float32)
             small = jnp.concatenate([small, fill], axis=0)
         small = small.T
-        here = slice(starts[c], starts[c] + widths[c])
         for k in (0, 1):
             at = base[k] - LANES
-            side_out[lap, k, :, here] = small[at : at + counts[k]]
+            strip_out[lap, where[k], :] = small[at : at + counts[k]]
         for k in (4, 5):
             at = base[k] - LANES
-            corner_out[lap, k - 4, :, here] = small[at : at + 1]
+            corner_out[lap, c, k - 4] = small[at : at + 1]
         for copy in copies(lap, c):
             copy.start()
 
@@ -204,13 +235,11 @@
     def outside(lap, c):
         size = cuts[c + 1] - cuts[c]
         h = size // 2
-        for copy in copies(lap, c):
-            copy.wait_recv()
-        half = slice(cuts[c] // 2, cuts[c + 1] // 2)
-        here = slice(starts[c], starts[c] + widths[c])
+        receive(lap, c)
+        where = places(c)
         left = lax.broadcasted_iota(jnp.int32, (h, LANES), 1) < length
-        above = rim_in[lap, 0, half, :]
-        below = rim_in[lap, 1, half, :]
+        above = strip_in[lap, where[2], :]
+        below = strip_in[lap, where[3], :]
         edge = jnp.concatenate(
             [
                 jnp.where(left, above, pltpu.roll(below, length, 1)),
@@ -219,13 +248,13 @@
             axis=0,
         )
         ends = base[4] - LANES
-        corners = jnp.zeros((LANES - ends, widths[c]), jnp.float32)
+        corners = jnp.zeros((LANES - ends, LANES), jnp.float32)
         place = lax.broadcasted_iota(jnp.int32, corners.shape, 0)
         for k in (4, 5):
-            value = jnp.broadcast_to(corner_in[lap, k - 4, :, here], corners.shape)
+            value = jnp.broadcast_to(corner_in[lap, c, k - 4], corners.shape)
             corners = jnp.where(place == base[k] - base[4], value, corners)
         small = jnp.concatenate(
-            [side_in[lap, 0, :, here], side_in[lap, 1, :, here], corners], axis=0
+            [strip_in[lap, where[0], :], strip_in[lap, where[1], :], corners], axis=0
         )
         high, low = split(jnp.concatenate([edge, small.T[:size]], axis=1))
         lhs = jnp.concatenate([high, low], axis=0)
@@ -235,15 +264,14 @@
 
     for row in gaps:
         flat[row : row + 1, :] = jnp.zeros((1, cell_count), jnp.float32)
-    loaded = set()
     for c in range(chunks):
-        need = {f for f, _, _, row in parts if row < cuts[c + 1]}
-        for f in sorted(need - loaded):
-            loads[f].wait()
+        for load, (f, n, first_use) in zip(loads, groups):
+            if first_use != c:
+                continue
+            load.wait()
             for g, level, size, row in parts:
-                if g == f:
-                    flat[row : row + size, :] = landed[f, level : level + size, :]
-        loaded |= need
+                if f <= g < f + n:
+                    flat[row : row + size, :] = landed[g, level : level + size, :]
         spread(flat[cuts[c] : cuts[c + 1], :], c)
         if c == 0:
             pl.semaphore_wait(barrier, len(targets))
@@ -348,10 +376,8 @@
 
     for step, c in ORDER:
         (inner, relay, finish)[step](c)
-    for lap in range(2):
-        for c in range(chunks):
-            for copy in copies(lap, c):
-                copy.wait_send()
+    pltpu.make_async_copy(strip_out, strip_out, send_sem.at[0]).wait()
+    pltpu.make_async_copy(corner_out, corner_out, send_sem.at[1]).wait()
 
 
 def shards(
@@ -363,10 +389,10 @@
     edge_count = dv_edge.shape[0]
     _, _, used = slots(length)
     halo = up(used, LANES)
-    _, _, rows = layout(fields_n, levels_n)
+    parts, _, rows = layout(fields_n, levels_n)
     cuts = bounds(rows)
     chunks = len(cuts) - 1
-    wide = sum(up(cuts[c + 1] - cuts[c], LANES) for c in range(chunks))
+    tall = strips(cuts)[-1]
     vmem = pl.BlockSpec(memory_space=pltpu.VMEM)
     hbm = pl.BlockSpec(memory_space=pltpu.HBM)
     return pl.pallas_call(
@@ -382,12 +408,10 @@
             pltpu.VMEM((2 * halo, cell_count), jnp.bfloat16),
             pltpu.VMEM((2 * rows, cell_count), jnp.bfloat16),
             pltpu.VMEM((cell_count, halo), jnp.bfloat16),
-            pltpu.VMEM((2, 2, rows // 2, 2 * length), jnp.float32),
-            pltpu.VMEM((2, 2, rows // 2, 2 * length), jnp.float32),
-            pltpu.VMEM((2, 2, CELLS_Y, wide), jnp.float32),
-            pltpu.VMEM((2, 2, CELLS_Y, wide), jnp.float32),
-            pltpu.VMEM((2, 2, 1, wide), jnp.float32),
-            pltpu.VMEM((2, 2, 1, wide), jnp.float32),
+            pltpu.VMEM((2, tall, LANES), jnp.float32),
+            pltpu.VMEM((2, tall, LANES), jnp.float32),
+            pltpu.VMEM((2, chunks, 2, 1, LANES), jnp.float32),
+            pltpu.VMEM((2, chunks, 2, 1, LANES), jnp.float32),
             pltpu.VMEM((8, LANES), jnp.int32),
             pltpu.VMEM((1, up(edge_count, LANES)), jnp.float32),
             pltpu.VMEM((1, up(edge_count, LANES)), jnp.int32),
@@ -402,10 +426,10 @@
             pltpu.VMEM(cell_area.shape, jnp.float32),
             pltpu.VMEM(level_coef.shape, jnp.float32),
             pltpu.VMEM((up(levels_n, 8), LANES), jnp.float32),
-            pltpu.SemaphoreType.DMA((fields_n,)),
+            pltpu.SemaphoreType.DMA((len(gather(parts, cuts)),)),
             pltpu.SemaphoreType.DMA((7,)),
-            pltpu.SemaphoreType.DMA((2, chunks, 6)),
-            pltpu.SemaphoreType.DMA((2, chunks, 6)),
+            pltpu.SemaphoreType.DMA((2,)),
+            pltpu.SemaphoreType.DMA((2, chunks, 2)),
         ],
         compiler_params=pltpu.CompilerParams(
             collective_id=0,

time: 31.8 us -> 30.7 us (0.965)
  Pallas kernels: 30.1 us -> 29.3 us
    pallas_call x1, Pallas kernels: 30.1 us -> 29.3 us  [shards(): pl.pallas_call(functools.partial(kernel, devices), out_shape=pltpu.VMEM(f...]
where the time goes in v3:
time: 30.7 us; the launch traced here: 30.6 us
  Pallas kernels  29.3 us (95%)
  local copies, waits for them, and re-layouts  1.31 us (4%)
    pallas_call x1, Pallas kernels, shards(): pl.pallas_call(functools.partial(kernel, devices), out_shape=pltpu.VMEM(f...  29.3 us
    unnamed x1, local copies, waits for them, and re-layouts  1.31 us

profile of v3, /device:TPU:0, one launch (start us, length us, event | category | flops | bytes accessed | tf_op | source)
XLA Modules:
  0.0 30.6 jit_solution(1157822291405801753)
XLA Ops:
  0.0 29.3 %diffuse.1 = f32[9,55,1024]{2,1,0:T(8,128)S(1)} custom-call(f32[9,55,1024]{2,1,0:T(8,128)} %field_hbm.1, f32[3232]{0:T(1024)} %dv_hbm.1, f32[3232]{0:T(1024)} %dc_hbm.1, s32[2,3232]{1,0:T(2,128)} %ends_hbm.1, s32[6,1024]{1,0:T(8,128)} %edges_hbm.1, s32[6,64]{1,0:T(8,128)} %send_hbm.1, f32[1024]{0:T(1024)} %area_hbm.1, f32[55]{0:T(128)} %level_hbm.1), custom_call_target="tpu_custom_call" | custom-call | tf_op jit(solution)/shard_map/diffuse/pallas_call | solution.py:398
  29.3 1.3 %copy.10 = f32[9,55,1024]{2,1,0:T(8,128)} copy(f32[9,55,1024]{2,1,0:T(8,128)S(1)} %diffuse.1) | data formatting | bytes 4055040

commit v4 on v3

--- a/solution.py
+++ b/solution.py
@@ -11,9 +11,10 @@
 BLOCK_ROW = 16
 OFFSETS = (1, -1, BLOCK_ROW, -BLOCK_ROW, BLOCK_ROW - 1, 1 - BLOCK_ROW)
 LANES = 128
+HALVES = 2
 UNIT = 16
-CUTS = (8, 8, 8, 7)
-ORDER = ((1, 0), (1, 1), (1, 2), (1, 3), (0, 0), (0, 1), (0, 2), (0, 3), (2, 0), (2, 1), (2, 2), (2, 3))
+CUTS = (7, 8, 8, 8)
+ORDER = ((1, 0), (1, 1), (2, 0), (1, 2), (2, 1), (1, 3), (2, 2), (2, 3), (0, 0), (0, 1), (0, 2), (0, 3), (3, 0), (3, 1), (3, 2))
 
 
 def up(value, step):
@@ -82,13 +83,90 @@
     return high, low
 
 
+def border(strip, corner_a, corner_b, size, length):
+    base, counts, _ = slots(length)
+    h = size // 2
+    left = lax.broadcasted_iota(jnp.int32, (h, LANES), 1) < length
+    above = strip[:h]
+    below = strip[h:size]
+    edge = jnp.concatenate(
+        [
+            jnp.where(left, above, pltpu.roll(below, length, 1)),
+            jnp.where(left, pltpu.roll(above, length, 1), below),
+        ],
+        axis=0,
+    )
+    corners = jnp.zeros((LANES - 2 * CELLS_Y, LANES), jnp.float32)
+    place = lax.broadcasted_iota(jnp.int32, corners.shape, 0)
+    for k, corner in ((4, corner_a), (5, corner_b)):
+        value = jnp.broadcast_to(corner, corners.shape)
+        corners = jnp.where(place == base[k] - base[4], value, corners)
+    small = jnp.concatenate([strip[size:], corners], axis=0)
+    high, low = split(jnp.concatenate([edge, small.T[:size]], axis=1))
+    return jnp.concatenate([high, low], axis=0)
+
+
+def split_fields(parts, cuts):
+    return min(f for f, _, size, row in parts if row + size > cuts[-2])
+
+
+def write_kernel(
+    length, parts, cuts, head_ref, tail_ref, sum_ref, rim, strip_ref, corner_ref, scale_ref,
+    out_hbm, rest, sems,
+):
+    lead = head_ref.shape[0]
+    fields_n, levels_n, cell_count = out_hbm.shape
+    start = cuts[-2]
+    size = cuts[-1] - start
+    halo = rim.shape[0] // 2
+    first = [
+        pltpu.make_async_copy(
+            head_ref.at[f], out_hbm.at[f], sems.at[0]
+        )
+        for f in range(lead)
+    ]
+    for copy in first:
+        copy.start()
+    for f, level, n, row in parts:
+        n = min(n, start - row)
+        if f >= lead and n > 0:
+            rest[f - lead, level : level + n, :] = tail_ref[f - lead, level : level + n, :]
+    lhs = border(strip_ref[...], corner_ref[0], corner_ref[1], size, length)
+    width = cell_count // HALVES
+    for k in range(HALVES):
+        here = slice(k * width, (k + 1) * width)
+        both = jnp.dot(lhs, rim[:halo, here], preferred_element_type=jnp.float32)
+        fine = jnp.dot(lhs[:size], rim[halo:, here], preferred_element_type=jnp.float32)
+        total = sum_ref[:, here] + (both[:size] + both[size:] + fine)
+        for f, level, n, row in parts:
+            lo = max(start, row)
+            hi = row + n
+            if lo >= hi:
+                continue
+            at = level + lo - row
+            scale = jnp.broadcast_to(scale_ref[at : at + hi - lo, 0:1], (hi - lo, width))
+            rest[f - lead, at : at + hi - lo, here] = total[lo - start : hi - start] * scale
+        there = pl.ds(k * width, width)
+        pltpu.make_async_copy(
+            rest.at[:, :, there], out_hbm.at[pl.ds(lead, fields_n - lead), :, there],
+            sems.at[1 + k],
+        ).start()
+    pltpu.make_async_copy(head_ref, out_hbm.at[pl.ds(0, lead)], sems.at[0]).wait()
+    for k in range(HALVES):
+        there = pl.ds(k * width, width)
+        pltpu.make_async_copy(
+            rest.at[:, :, there], out_hbm.at[pl.ds(lead, fields_n - lead), :, there],
+            sems.at[1 + k],
+        ).wait()
+
+
 def kernel(
     devices,
     field_hbm, dv_hbm, dc_hbm, ends_hbm, edges_hbm, send_hbm, area_hbm, level_hbm,
-    out_ref,
-    landed, flat, first, matrix, rim, pair, selector, strip_out, strip_in,
+    head_ref, tail_ref, sum_ref, rim, last_strip, last_corner, scale_ref,
+    landed, flat, first, matrix, pair, selector, strip_out, strip_in,
     corner_out, corner_in, lists, weight, packed, index, near_ref, coef_ref,
-    dv_ref, dc_ref, ends_ref, edges_ref, send_ref, area_ref, level_ref, scale_ref,
+    dv_ref, dc_ref, ends_ref, edges_ref, send_ref, area_ref, level_ref,
     load_sem, table_sem, send_sem, recv_sem,
 ):
     fields_n, levels_n, cell_count = field_hbm.shape
@@ -119,8 +197,9 @@
         )
         for i, (f, n, _) in enumerate(groups)
     ]
-    for load in loads:
-        load.start()
+    for load, (_, _, first_use) in zip(loads, groups):
+        if first_use == 0:
+            load.start()
     pairs = (
         (dv_hbm, dv_ref), (dc_hbm, dc_ref), (ends_hbm, ends_ref), (edges_hbm, edges_ref),
         (area_hbm, area_ref), (level_hbm, level_ref),
@@ -128,9 +207,6 @@
     tables = [
         pltpu.make_async_copy(a, b, table_sem.at[i + 1]) for i, (a, b) in enumerate(pairs)
     ]
-    for load in tables:
-        load.start()
-
     send_load.wait()
     lists[0:6, 0:length] = send_ref[...]
     table = lists[...]
@@ -233,37 +309,14 @@
         return both[:size] + both[size:] + fine
 
     def outside(lap, c):
+        receive(lap, c)
         size = cuts[c + 1] - cuts[c]
-        h = size // 2
-        receive(lap, c)
-        where = places(c)
-        left = lax.broadcasted_iota(jnp.int32, (h, LANES), 1) < length
-        above = strip_in[lap, where[2], :]
-        below = strip_in[lap, where[3], :]
-        edge = jnp.concatenate(
-            [
-                jnp.where(left, above, pltpu.roll(below, length, 1)),
-                jnp.where(left, pltpu.roll(above, length, 1), below),
-            ],
-            axis=0,
-        )
-        ends = base[4] - LANES
-        corners = jnp.zeros((LANES - ends, LANES), jnp.float32)
-        place = lax.broadcasted_iota(jnp.int32, corners.shape, 0)
-        for k in (4, 5):
-            value = jnp.broadcast_to(corner_in[lap, c, k - 4], corners.shape)
-            corners = jnp.where(place == base[k] - base[4], value, corners)
-        small = jnp.concatenate(
-            [strip_in[lap, where[0], :], strip_in[lap, where[1], :], corners], axis=0
-        )
-        high, low = split(jnp.concatenate([edge, small.T[:size]], axis=1))
-        lhs = jnp.concatenate([high, low], axis=0)
+        strip = strip_in[lap, starts[c] : starts[c + 1], :]
+        lhs = border(strip, corner_in[lap, c, 0], corner_in[lap, c, 1], size, length)
         both = jnp.dot(lhs, rim[:halo, :], preferred_element_type=jnp.float32)
-        fine = jnp.dot(high, rim[halo:, :], preferred_element_type=jnp.float32)
+        fine = jnp.dot(lhs[:size], rim[halo:, :], preferred_element_type=jnp.float32)
         return both[:size] + both[size:] + fine
 
-    for row in gaps:
-        flat[row : row + 1, :] = jnp.zeros((1, cell_count), jnp.float32)
     for c in range(chunks):
         for load, (f, n, first_use) in zip(loads, groups):
             if first_use != c:
@@ -272,6 +325,12 @@
             for g, level, size, row in parts:
                 if f <= g < f + n:
                     flat[row : row + size, :] = landed[g, level : level + size, :]
+        if c == 0:
+            for load, (_, _, first_use) in zip(loads, groups):
+                if first_use:
+                    load.start()
+            for load in tables:
+                load.start()
         spread(flat[cuts[c] : cuts[c + 1], :], c)
         if c == 0:
             pl.semaphore_wait(barrier, len(targets))
@@ -350,9 +409,12 @@
             rim[r * LANES : (r + 1) * LANES, here] = high
             rim[halo + r * LANES : halo + (r + 1) * LANES, here] = low
 
+    def start(c):
+        part = slice(cuts[c], cuts[c + 1])
+        first[part, :] = own(c) - flat[part, :] * coef_ref[6:7, :]
+
     def relay(c):
         part = slice(cuts[c], cuts[c + 1])
-        first[part, :] = own(c) - flat[part, :] * coef_ref[6:7, :]
         result = first[part, :] + outside(0, c)
         first[part, :] = result
         spread(result, c)
@@ -361,6 +423,8 @@
     def inner(c):
         part = slice(cuts[c], cuts[c + 1])
         flat[part, :] = own(c) - first[part, :] * coef_ref[6:7, :]
+
+    lead = head_ref.shape[0]
 
     def finish(c):
         part = slice(cuts[c], cuts[c + 1])
@@ -372,10 +436,16 @@
                 continue
             at = level + lo - row
             scale = jnp.broadcast_to(scale_ref[at : at + hi - lo, 0:1], (hi - lo, cell_count))
-            out_ref[f, at : at + hi - lo, :] = flat[lo:hi, :] * scale
+            where, g = (head_ref, f) if f < lead else (tail_ref, f - lead)
+            where[g, at : at + hi - lo, :] = flat[lo:hi, :] * scale
 
     for step, c in ORDER:
-        (inner, relay, finish)[step](c)
+        (inner, start, relay, finish)[step](c)
+    c = chunks - 1
+    sum_ref[...] = flat[cuts[c] : cuts[c + 1], :]
+    receive(1, c)
+    last_strip[...] = strip_in[1, starts[c] : starts[c + 1], :]
+    last_corner[...] = corner_in[1, c]
     pltpu.make_async_copy(strip_out, strip_out, send_sem.at[0]).wait()
     pltpu.make_async_copy(corner_out, corner_out, send_sem.at[1]).wait()
 
@@ -395,17 +465,35 @@
     tall = strips(cuts)[-1]
     vmem = pl.BlockSpec(memory_space=pltpu.VMEM)
     hbm = pl.BlockSpec(memory_space=pltpu.HBM)
-    return pl.pallas_call(
+    lead = split_fields(parts, cuts)
+    last = cuts[-1] - cuts[-2]
+    shapes = (
+        pltpu.VMEM((lead, levels_n, cell_count), jnp.float32),
+        pltpu.VMEM((fields_n - lead, levels_n, cell_count), jnp.float32),
+        pltpu.VMEM((last, cell_count), jnp.float32),
+        pltpu.VMEM((2 * halo, cell_count), jnp.bfloat16),
+        pltpu.VMEM((last + 2 * CELLS_Y, LANES), jnp.float32),
+        pltpu.VMEM((2, 1, LANES), jnp.float32),
+        pltpu.VMEM((up(levels_n, 8), LANES), jnp.float32),
+    )
+    held = (
+        fields_n * up(levels_n, 8) * cell_count * 4
+        + last * cell_count * 4
+        + 4 * halo * cell_count
+        + (last + 2 * CELLS_Y) * LANES * 4
+        + 2 * 8 * LANES * 4
+        + up(levels_n, 8) * LANES * 4
+    )
+    results = pl.pallas_call(
         functools.partial(kernel, devices),
-        out_shape=pltpu.VMEM(field.shape, jnp.float32),
+        out_shape=shapes,
         in_specs=[hbm] * 8,
-        out_specs=vmem,
+        out_specs=(vmem,) * len(shapes),
         scratch_shapes=[
             pltpu.VMEM(field.shape, jnp.float32),
             pltpu.VMEM((rows, cell_count), jnp.float32),
             pltpu.VMEM((rows, cell_count), jnp.float32),
             pltpu.VMEM((2 * cell_count, cell_count), jnp.bfloat16),
-            pltpu.VMEM((2 * halo, cell_count), jnp.bfloat16),
             pltpu.VMEM((2 * rows, cell_count), jnp.bfloat16),
             pltpu.VMEM((cell_count, halo), jnp.bfloat16),
             pltpu.VMEM((2, tall, LANES), jnp.float32),
@@ -425,7 +513,6 @@
             pltpu.VMEM(send_cells.shape, jnp.int32),
             pltpu.VMEM(cell_area.shape, jnp.float32),
             pltpu.VMEM(level_coef.shape, jnp.float32),
-            pltpu.VMEM((up(levels_n, 8), LANES), jnp.float32),
             pltpu.SemaphoreType.DMA((len(gather(parts, cuts)),)),
             pltpu.SemaphoreType.DMA((7,)),
             pltpu.SemaphoreType.DMA((2,)),
@@ -434,12 +521,24 @@
         compiler_params=pltpu.CompilerParams(
             collective_id=0,
             has_side_effects=True,
-            vmem_limit_bytes=67043328 - fields_n * up(levels_n, 8) * cell_count * 4,
+            vmem_limit_bytes=67043328 - up(held, 1024),
         ),
         name="diffuse",
     )(
         field, dv_edge, dc_edge, cells_on_edge, edges_on_cell, send_cells, cell_area, level_coef
     )
+    return pl.pallas_call(
+        functools.partial(write_kernel, length, parts, cuts),
+        out_shape=jax.ShapeDtypeStruct(field.shape, jnp.float32),
+        in_specs=[vmem] * len(shapes),
+        out_specs=hbm,
+        scratch_shapes=[
+            pltpu.VMEM((fields_n - lead, levels_n, cell_count), jnp.float32),
+            pltpu.SemaphoreType.DMA((1 + HALVES,)),
+        ],
+        compiler_params=pltpu.CompilerParams(vmem_limit_bytes=32 * 1024 * 1024),
+        name="write",
+    )(*results)
 
 
 def solution(mesh):

time: 30.7 us -> 30.1 us (0.980)
  local copies, waits for them, and re-layouts: 1.31 us -> 0 us
  Pallas kernels: 29.3 us -> 29.9 us
    unnamed x1 -> x0, local copies, waits for them, and re-layouts: 1.31 us -> none
    pallas_call x1 -> x2, Pallas kernels: 29.3 us -> 29.9 us  [the longest x1 28.6 us: shards(): pl.pallas_call(functools.partial(kernel, devices), out_shape=shapes, in_s...]
where the time goes in v4:
time: 30.1 us; the launch traced here: 30 us
  Pallas kernels  29.9 us (99%)
    pallas_call x1, Pallas kernels, shards(): pl.pallas_call(functools.partial(kernel, devices), out_shape=shapes, in_s...  28.6 us
    pallas_call x1, Pallas kernels, shards(): pl.pallas_call(functools.partial(write_kernel, length, parts, cuts), out_...  1.33 us

profile of v4, /device:TPU:0, one launch (start us, length us, event | category | flops | bytes accessed | tf_op | source)
XLA Modules:
  0.0 30.0 jit_solution(18043894424990587124)
XLA Ops:
  0.0 28.6 %diffuse.1 = (f32[6,55,1024]{2,1,0:T(8,128)S(1)}, f32[3,55,1024]{2,1,0:T(8,128)S(1)}, f32[128,1024]{1,0:T(8,128)S(1)}, bf16[512,1024]{1,0:T(8,128)(2,1)S(1)}, f3...) custom-call(f32[9,55,1024]{2,1,0:T(8,128)} %field_hbm.1, f32[3232]{0:T(1024)} %dv_hbm.1, ...), custom_call_target="tpu_custom_call" | custom-call | tf_op jit(solution)/shard_map/diffuse/pallas_call | solution.py:487
  28.6 1.3 %write.1 = f32[9,55,1024]{2,1,0:T(8,128)} custom-call(f32[6,55,1024]{2,1,0:T(8,128)S(1)} %get-tuple-element.12.head_ref, f32[3,55,1024]{2,1,0:T(8,128)S(1)} %get-tuple-element.13.tail_ref, f32[128,1024]{1,0:T(8,128)S(1)} %get-tuple-element.14.sum_ref, bf16[512,1024]{1,0:T(8,128)(2,1)S(1)} %get-tuple-element.15.rim, ...), custom_call_target="tpu_custom_call" | custom-call | tf_op jit(solution)/shard_map/write/pallas_call | solution.py:530

commit v5 on v4

--- a/solution.py
+++ b/solution.py
@@ -13,8 +13,8 @@
 LANES = 128
 HALVES = 2
 UNIT = 16
-CUTS = (7, 8, 8, 8)
-ORDER = ((1, 0), (1, 1), (2, 0), (1, 2), (2, 1), (1, 3), (2, 2), (2, 3), (0, 0), (0, 1), (0, 2), (0, 3), (3, 0), (3, 1), (3, 2))
+CUTS = (8, 8, 8, 7)
+ORDER = ((1, 0), (1, 1), (2, 0), (1, 2), (2, 1), (1, 3), (2, 2), (0, 0), (2, 3), (0, 1), (0, 2), (0, 3), (3, 0), (3, 1), (3, 2))
 
 
 def up(value, step):

time: 30.1 us -> 30.3 us (level)
  no operation moved by 1% of the time
where the time goes in v5:
time: 30.3 us; the launch traced here: 30.2 us
  Pallas kernels  30.2 us (100%)
    pallas_call x1, Pallas kernels, shards(): pl.pallas_call(functools.partial(kernel, devices), out_shape=shapes, in_s...  28.8 us
    pallas_call x1, Pallas kernels, shards(): pl.pallas_call(functools.partial(write_kernel, length, parts, cuts), out_...  1.33 us

profile of v5, /device:TPU:0, one launch (start us, length us, event | category | flops | bytes accessed | tf_op | source)
XLA Modules:
  0.0 30.2 jit_solution(6262899244693803719)
XLA Ops:
  0.0 28.8 %diffuse.1 = (f32[6,55,1024]{2,1,0:T(8,128)S(1)}, f32[3,55,1024]{2,1,0:T(8,128)S(1)}, f32[112,1024]{1,0:T(8,128)S(1)}, bf16[512,1024]{1,0:T(8,128)(2,1)S(1)}, f3...) custom-call(f32[9,55,1024]{2,1,0:T(8,128)} %field_hbm.1, f32[3232]{0:T(1024)} %dv_hbm.1, ...), custom_call_target="tpu_custom_call" | custom-call | tf_op jit(solution)/shard_map/diffuse/pallas_call | solution.py:487
  28.8 1.3 %write.1 = f32[9,55,1024]{2,1,0:T(8,128)} custom-call(f32[6,55,1024]{2,1,0:T(8,128)S(1)} %get-tuple-element.12.head_ref, f32[3,55,1024]{2,1,0:T(8,128)S(1)} %get-tuple-element.13.tail_ref, f32[112,1024]{1,0:T(8,128)S(1)} %get-tuple-element.14.sum_ref, bf16[512,1024]{1,0:T(8,128)(2,1)S(1)} %get-tuple-element.15.rim, ...), custom_call_target="tpu_custom_call" | custom-call | tf_op jit(solution)/shard_map/write/pallas_call | solution.py:530
